TPU v7x, 32 devices: a whole 2x2x4 slice. The times are simulated.
32 devices in a mesh: dp: 8 (over z, y), expert: 2 (over core), tensor: 2 (over x).
Axes of the slice: x: 2, y: 2, z: 4, core: 2. Of those that a mesh axis runs over, the one named last changes fastest.
Arguments:
- dense_act: bfloat16 [2, 32, 512, 3584], P(None, 'dp', 'expert', 'tensor'), may hold values from -6 to 6
- dense_cot: bfloat16 [2, 32, 512, 3584], P(None, 'dp', ('expert', 'tensor')), may hold values from -6 to 6
- dense_proj_in: bfloat16 [2, 3584, 128], P(None, 'tensor'), may hold values from -0.09375 to 0.09375
- dense_proj_out: bfloat16 [2, 3584, 128], replicated, may hold values from -0.09375 to 0.09375
- expert_act: bfloat16 [32, 8, 64, 2560], P('dp', 'expert', None, 'tensor'), may hold values from -6 to 6
- expert_cot: bfloat16 [32, 8, 64, 3584], P('dp', 'expert', 'tensor'), may hold values from -6 to 6
- expert_proj_in: bfloat16 [2560, 128], P('tensor'), may hold values from -0.125 to 0.125
- expert_proj_out: bfloat16 [3584, 128], replicated, may hold values from -0.09375 to 0.09375
- dense_valid: float32 [2, 128, 128], replicated, may hold values from -0.0012207031 to 0.0012207031
- expert_valid: float32 [8, 128, 128], P('expert'), may hold values from -0.0012207031 to 0.0012207031
- domain_ids: int32 [32], P('dp'), may hold values from 0 to 63
- prior_mix: float32 [64], replicated, may hold values from 0.002 to 0.05
Outputs:
- log_mixture_weights: float32 [64], P('dp')
All inputs are finite; a program needn't handle non-finite values.
Results may differ from a plain program's by a relative error of at most 0.0003.
Values sent between devices are 32-bit elements; how exact they have to be, the bound alone decides.
A program may use at most 128 MiB of HBM per device.

v0:
```python
import jax
import jax.numpy as jnp
from jax import lax
from jax.sharding import PartitionSpec as P


def per_device(
    dense_act,
    dense_cot,
    dense_proj_in,
    dense_proj_out,
    expert_act,
    expert_cot,
    expert_proj_in,
    expert_proj_out,
    dense_valid,
    expert_valid,
    domain_ids,
    prior_mix,
):
    block = dense_act
    dense_update_vector = lax.psum_scatter(
        jnp.einsum("lmtd,ldr->tlmr", block, dense_proj_in, preferred_element_type=jnp.float32),
        "tensor",
        scatter_dimension=0,
        tiled=True,
    )
    dense_weight_matrix = jnp.einsum(
        "lmtd,ldr->tlmr", dense_cot, dense_proj_out, preferred_element_type=jnp.float32
    )
    dense_portion = jnp.einsum(
        "fquy,fquh->quyh", dense_update_vector, dense_weight_matrix, precision=lax.Precision.HIGHEST
    )
    block = expert_act
    expert_u = lax.psum_scatter(
        jnp.einsum("mecf,fr->cmer", block, expert_proj_in, preferred_element_type=jnp.float32),
        "tensor",
        scatter_dimension=0,
        tiled=True,
    )
    expert_weight_matrix = jnp.einsum(
        "mecd,dr->cmer", expert_cot, expert_proj_out, preferred_element_type=jnp.float32
    )
    expert_part = jnp.einsum(
        "cmer,cmes->mers", expert_u, expert_weight_matrix, precision=lax.Precision.HIGHEST
    )
    dense_full = lax.psum(dense_portion, ("expert", "tensor"))
    dense_score = jnp.sum(dense_full * dense_valid[:, None], axis=(0, 2, 3))
    expert_full = lax.psum(expert_part, "tensor")
    expert_local = jnp.sum(expert_full * expert_valid[None], axis=(1, 2, 3))
    score = dense_score + lax.psum(expert_local, "expert")
    domains = prior_mix.shape[0]
    onehot = (domain_ids[:, None] == jnp.arange(domains, dtype=jnp.int32)[None, :]).astype(
        jnp.float32
    )
    domain_part = jnp.dot(score, onehot, precision=lax.Precision.HIGHEST)
    share_tally_count = domains // lax.axis_size("dp")
    first_domain = lax.axis_index("dp") * share_tally_count
    previous_domain_share = lax.dynamic_slice_in_dim(prior_mix, first_domain, share_tally_count, 0)
    domain_total = lax.psum(domain_part, "dp")
    spread = jnp.sqrt(jnp.mean(domain_total * domain_total) + 1e-06)
    z_value = domain_total / spread
    mass = jnp.sum(prior_mix * jnp.exp(0.5 * z_value))
    z_share = lax.dynamic_slice_in_dim(z_value, first_domain, share_tally_count, 0)
    return jnp.log(previous_domain_share) + 0.5 * z_share - jnp.log(mass)


def solution(mesh):
    placed = (
        P(None, "dp", "expert", "tensor"),
        P(None, "dp", ("expert", "tensor"), None),
        P(None, "tensor", None),
        P(),
        P("dp", "expert", None, "tensor"),
        P("dp", "expert", "tensor", None),
        P("tensor", None),
        P(),
        P(),
        P("expert", None, None),
        P("dp"),
        P(),
    )
    return jax.shard_map(per_device, mesh=mesh, in_specs=placed, out_specs=P("dp"), check_vma=False)
```

profile of v0, /device:TPU:0, one launch (start us, length us, event | category | flops | bytes accessed | tf_op | source)
XLA Modules:
  0.0 206.4 jit_solution(693878961875852554)
XLA Ops:
  6.5 0.0 copy-start
  6.5 0.0 copy-start.3
  6.5 0.0 all-reduce.9.cloned.1.call-start
  6.5 1.7 copy-done
  8.3 1.8 convolution_bitcast_fusion.1
  10.1 1.1 copy.18
  11.2 0.0 all-reduce.9.cloned.1.call-update
  11.3 0.0 reduce-scatter.4.cloned.1.call-start
  11.3 0.0 copy-done.3
  11.3 5.6 %convolution_bitcast_fusion = f32[256,2,4,128]{0,3,2,1:T(8,128)S(1)} fusion(bf16[2,4,256,1792]{3,2,1,0:T(8,128)(2,1)} %param.12, bf16[2,1792,128]{2,1,0:T(8,128)(2,1)S(1)} %copy-done.3), kind=kOutput, calls=%fused_computation.2 | convolution fusion | flops 939524096 | bytes 9306112 | tf_op jit(solution)/shard_map/lmtd,ldr->tlmr/dot_general | solution.py:23
  16.9 26.2 %copy.29 = f32[256,2,4,128]{2,3,1,0:T(8,128)} copy(f32[256,2,4,128]{0,3,2,1:T(8,128)S(1)} %convolution_bitcast_fusion) | data formatting | bytes 2097152
  43.2 0.0 copy-start.9
  43.2 0.0 copy-start.7
  43.2 29.4 %reshape.9 = f32[256,1024]{1,0:T(8,128)} reshape(f32[256,2,128,4]{3,2,1,0:T(8,128)} %bitcast.46) | data formatting | bytes 2097152
  72.5 0.0 reduce-scatter.4.cloned.1.call-update
  72.6 0.0 all-reduce.7.cloned.1.call-start
  72.6 0.0 copy-done.9
  72.6 0.6 dynamic-slice
  73.9 0.0 copy-done.7
  73.9 0.0 copy-start.2
  73.9 3.3 %fusion.6 = f32[128,4,4,32]{0,3,2,1:T(8,128)S(1)} fusion(bf16[4,4,32,3584]{3,2,1,0:T(8,128)(2,1)} %param.17, bf16[3584,128]{1,0:T(8,128)(2,1)S(1)} %copy-done.7), kind=kOutput, calls=%fused_computation.8 | convolution fusion | flops 469762048 | bytes 4849664 | tf_op jit(solution)/shard_map/mecd,dr->cmer/dot_general | solution.py:41
  77.2 0.0 all-reduce.9.cloned.1.call-done
  77.2 1.0 constant_dynamic-slice_fusion
  78.2 2.8 %fusion.9 = f32[4,4,128,128]{3,2,1,0:T(8,128)} fusion(f32[128,4,4,32]{0,3,2,1:T(8,128)S(1)} %fusion.6, f32[32,4,4,128]{3,2,1,0:T(4,128)S(1)} %constant_dynamic-slice_fusion), kind=kOutput, calls=%fused_computation.12 | convolution fusion | flops 100663296 | bytes 1572864 | tf_op jit(solution)/shard_map/cmer,cmes->mers/dot_general | solution.py:44
  81.0 0.0 all-reduce.7.cloned.1.call-update
  81.0 0.2 all-reduce.5.cloned.1.call-start
  81.3 0.0 copy-done.2
  81.3 5.6 %fusion.2 = f32[128,2,4,128]{0,3,2,1:T(8,128)S(1)} fusion(bf16[2,4,128,3584]{3,2,1,0:T(8,128)(2,1)} %param.13, bf16[2,3584,128]{2,1,0:T(8,128)(2,1)S(1)} %copy-done.2), kind=kOutput, calls=%fused_computation.3 | convolution fusion | flops 939524096 | bytes 9699328 | tf_op jit(solution)/shard_map/lmtd,ldr->tlmr/dot_general | solution.py:28
  86.9 8.9 %reduce-scatter.4.cloned.1.call-done = f32[128,1024]{1,0:T(8,128)} async-done(((f32[256,1024]{1,0:T(8,128)}), f32[128,1024]{1,0:T(8,128)}) %reduce-scatter.4.cloned.1.call-update) | async-done | bytes 524304
  95.8 19.5 %reshape.10 = f32[128,2,128,4]{3,2,1,0:T(8,128)} reshape(f32[128,1024]{1,0:T(8,128)} %reduce-scatter.4.cloned.1.call-done) | data formatting | bytes 1048576
  115.3 0.0 copy-start.4
  115.3 0.0 copy-start.5
  115.3 0.0 copy-start.1
  115.3 13.2 %copy.16 = f32[128,2,4,128]{0,3,2,1:T(8,128)} copy(f32[128,2,4,128]{2,3,1,0:T(8,128)} %bitcast.47) | data formatting | bytes 1048576 | tf_op jit(solution)/shard_map/reduce_scatter | solution.py:22
  128.5 0.0 copy-start.8
  128.5 0.0 copy-start.6
  128.5 3.1 %fusion.12 = f32[2,4,128,128]{3,2,1,0:T(8,128)} fusion(f32[128,2,4,128]{0,3,2,1:T(8,128)} %copy.16, f32[128,2,4,128]{0,3,2,1:T(8,128)S(1)} %fusion.2), kind=kOutput, calls=%fused_computation.22 | convolution fusion | flops 201326592 | bytes 1572864 | tf_op jit(solution)/shard_map/fquy,fquh->quyh/dot_general | solution.py:31
  131.6 0.0 all-reduce.5.cloned.1.call-update
  131.6 6.7 %all-reduce.7.cloned.1.call-done = f32[4,4,128,128]{3,2,1,0:T(8,128)} async-done(((f32[4,4,128,128]{3,2,1,0:T(8,128)}), f32[4,4,128,128]{3,2,1,0:T(8,128)}) %all-reduce.7.cloned.1.call-update) | async-done | bytes 1048592 | tf_op jit(solution)/shard_map/psum | solution.py:49
  138.3 0.0 copy-done.4
  138.3 1.4 multiply_reduce_fusion
  139.7 2.4 %psum.30 = f32[4]{0:T(128)S(1)} all-reduce(f32[4]{0:T(128)S(1)} %multiply_reduce_fusion), channel_id=1, replica_groups=mesh['dp'=8,'expert'=2,'tensor'=2] {'expert'}, use_global_device_ids=true, to_apply=%region_6.0 | all-reduce | flops 4 | bytes 32 | tf_op jit(solution)/shard_map/psum | solution.py:51
  142.1 31.8 %all-reduce.5.cloned.1.call-done = f32[2,4,128,128]{3,2,1,0:T(8,128)} async-done(((f32[2,4,128,128]{3,2,1,0:T(8,128)}), f32[2,4,128,128]{3,2,1,0:T(8,128)}) %all-reduce.5.cloned.1.call-update) | async-done | bytes 524304 | tf_op jit(solution)/shard_map/psum | solution.py:47
  173.9 0.0 copy-done.5
  173.9 1.2 multiply_reduce_fusion.1
  175.1 0.0 copy-done.8
  175.1 0.2 convolution_bitcast_fusion.2
  175.3 21.3 %psum.31 = f32[64]{0:T(128)S(1)} all-reduce(f32[64]{0:T(128)S(1)} %convolution_bitcast_fusion.2), channel_id=1, replica_groups=mesh['dp'=8,'expert'=2,'tensor'=2] {'dp'}, use_global_device_ids=true, to_apply=%region_7.0 | all-reduce | flops 64 | bytes 512 | tf_op jit(solution)/shard_map/psum | solution.py:60
  196.7 0.6 multiply_reduce_fusion.3
  198.0 0.0 copy-done.6
  198.0 0.6 multiply_reduce_fusion.2
  199.3 0.6 add_subtract_fusion
  199.9 0.0 copy-done.1
Async XLA Ops:
  6.5 1.7 copy-start
  6.5 4.8 %copy-start.3 = (bf16[2,1792,128]{2,1,0:T(8,128)(2,1)S(1)}, bf16[2,1792,128]{2,1,0:T(8,128)(2,1)}, u32[]{:S(2)}) copy-start(bf16[2,1792,128]{2,1,0:T(8,128)(2,1)} %param.14) | copy-start | bytes 2752516
  6.5 70.6 %all-reduce.9.cloned.1.call-start = ((), (), s32[]{:S(2)}) async-start(), calls=%async_computation.4 | async-start | bytes 1048576
  11.3 84.6 %reduce-scatter.4.cloned.1.call-start = ((), (), s32[]{:S(2)}) async-start(), calls=%async_computation.3 | async-start | bytes 1572864
  43.2 29.4 %copy-start.9 = (u32[32]{0:T(128)S(1)}, u32[32]{0:T(128)}, u32[]{:S(2)}) copy-start(u32[32]{0:T(128)} %constant.29) | copy-start | bytes 388
  43.2 30.7 %copy-start.7 = (bf16[3584,128]{1,0:T(8,128)(2,1)S(1)}, bf16[3584,128]{1,0:T(8,128)(2,1)}, u32[]{:S(2)}) copy-start(bf16[3584,128]{1,0:T(8,128)(2,1)} %param.19) | copy-start | bytes 2752516
  72.6 65.7 %all-reduce.7.cloned.1.call-start = ((), (), s32[]{:S(2)}) async-start(), calls=%async_computation.2 | async-start | bytes 2097152 | tf_op jit(solution)/shard_map/psum | solution.py:49
  73.9 7.4 %copy-start.2 = (bf16[2,3584,128]{2,1,0:T(8,128)(2,1)S(1)}, bf16[2,3584,128]{2,1,0:T(8,128)(2,1)}, u32[]{:S(2)}) copy-start(bf16[2,3584,128]{2,1,0:T(8,128)(2,1)} %param.15) | copy-start | bytes 5505028
  81.0 92.9 %all-reduce.5.cloned.1.call-start = ((), (), s32[]{:S(2)}) async-start(), calls=%async_computation.1 | async-start | bytes 1048576 | tf_op jit(solution)/shard_map/psum | solution.py:47
  115.3 22.9 %copy-start.4 = (f32[4,128,128]{2,1,0:T(8,128)S(1)}, f32[4,128,128]{2,1,0:T(8,128)}, u32[]{:S(2)}) copy-start(f32[4,128,128]{2,1,0:T(8,128)} %param.21) | copy-start | bytes 786436
  115.3 58.6 %copy-start.5 = (f32[2,128,128]{2,1,0:T(8,128)S(1)}, f32[2,128,128]{2,1,0:T(8,128)}, u32[]{:S(2)}) copy-start(f32[2,128,128]{2,1,0:T(8,128)} %param.20) | copy-start | bytes 393220
  115.3 84.5 %copy-start.1 = (bf16[4,4,64,1280]{3,2,1,0:T(8,128)(2,1)S(1)}, bf16[4,4,64,1280]{3,2,1,0:T(8,128)(2,1)}, u32[]{:S(2)}) copy-start(bf16[4,4,64,1280]{3,2,1,0:T(8,128)(2,1)} %param.16) | copy-start | bytes 7864324
  128.5 46.6 %copy-start.8 = (s32[4]{0:T(128)S(1)}, s32[4]{0:T(128)}, u32[]{:S(2)}) copy-start(s32[4]{0:T(128)} %param.22) | copy-start | bytes 52
  128.5 69.5 %copy-start.6 = (f32[64]{0:T(128)S(1)}, f32[64]{0:T(128)}, u32[]{:S(2)}) copy-start(f32[64]{0:T(128)} %param.23) | copy-start | bytes 772
Sparse Core Ops, SparseCore 0:
  11.4 31.3 all-reduce.8
  72.7 23.1 reduce-scatter.3
  98.1 40.0 all-reduce.6
  140.5 33.4 all-reduce.4
where the time goes:
time: 207 us; the launch traced here: 206 us
  local copies, waits for them, and re-layouts  92.7 us (45%)
  waiting for transfers between devices  47.4 us (23%)
  blocking collectives  23.8 us (11%)
  matrix products  22.5 us (11%)
  between operations  15.3 us (7%)
  other arithmetic  4.44 us (2%)
    unnamed x25, local copies, waits for them, and re-layouts  78.4 us
    psum x1, waiting for transfers between devices, per_device(): dense_full = lax.psum(dense_portion, ('expert', 'tensor'))  31.8 us
    psum x1, blocking collectives, per_device(): domain_total = lax.psum(domain_part, 'dp')  21.3 us
    reduce_scatter x1, local copies, waits for them, and re-layouts, per_device(): lax.psum_scatter(jnp.einsum('lmtd,ldr->tlmr', block, dense_proj_in, prefe...  13.2 us
    unnamed x6, waiting for transfers between devices  8.98 us
    psum x1, waiting for transfers between devices, per_device(): expert_full = lax.psum(expert_part, 'tensor')  6.66 us
    dot_general x1, matrix products, per_device(): jnp.einsum('lmtd,ldr->tlmr', dense_cot, dense_proj_out, preferred_element...  5.64 us
    dot_general x1, matrix products, per_device(): jnp.einsum('lmtd,ldr->tlmr', block, dense_proj_in, preferred_element_type...  5.62 us
  transfers between devices with their start and end apart: 4, of which 3 were waited for; matrix products, arithmetic and copies ran while one was open for 54% of the time, Pallas kernels for 0%

commit v1 on v0

--- a/solution.py
+++ b/solution.py
@@ -44,7 +44,7 @@
     expert_part = jnp.einsum(
         "cmer,cmes->mers", expert_u, expert_weight_matrix, precision=lax.Precision.HIGHEST
     )
-    dense_full = lax.psum(dense_portion, ("expert", "tensor"))
+    dense_full = jnp.sum(lax.all_gather(dense_portion, ("expert", "tensor")), axis=0)
     dense_score = jnp.sum(dense_full * dense_valid[:, None], axis=(0, 2, 3))
     expert_full = lax.psum(expert_part, "tensor")
     expert_local = jnp.sum(expert_full * expert_valid[None], axis=(1, 2, 3))

time: 207 us -> 165 us (0.80)
  local copies, waits for them, and re-layouts: 92.7 us -> 4.46 us
  waiting for transfers between devices: 47.4 us -> 92.1 us
    unnamed x25 -> x16, local copies, waits for them, and re-layouts: 78.4 us -> 3.32 us
    psum x1, waiting for transfers between devices: 6.66 us -> 39.3 us  [per_device(): expert_full = lax.psum(expert_part, 'tensor')]
    psum x1 -> x0, waiting for transfers between devices: 31.8 us -> none  [per_device(): dense_full = lax.psum(dense_portion, ('expert', 'tensor'))]
    all_gather x0 -> x1, waiting for transfers between devices: none -> 20.1 us  [per_device(): lax.all_gather(dense_portion, ('expert', 'tensor'))]
    reduce_scatter x1 -> x0, local copies, waits for them, and re-layouts: 13.2 us -> none  [per_device(): lax.psum_scatter(jnp.einsum('lmtd,ldr->tlmr', block, dense_proj_in, prefe...]
    reduce_scatter x0 -> x1, waiting for transfers between devices: none -> 12.5 us  [per_device(): lax.psum_scatter(jnp.einsum('lmtd,ldr->tlmr', block, dense_proj_in, prefe...]
    unnamed x6 -> x5, waiting for transfers between devices: 8.98 us -> 20.1 us
  transfers between devices with their start and end apart: 4 -> 4, of which waited for: 3 -> 4; matrix products, arithmetic and copies ran while one was open for 54% -> 15% of each run, Pallas kernels for 0% -> 0%
where the time goes in v1:
time: 165 us
  waiting for transfers between devices  92.1 us (56%)
  matrix products  24.1 us (15%)
  blocking collectives  23.8 us (14%)
  between operations  15.3 us (9%)
  other arithmetic  5.16 us (3%)
  local copies, waits for them, and re-layouts  4.46 us (3%)
    psum x1, waiting for transfers between devices, per_device(): expert_full = lax.psum(expert_part, 'tensor')  39.3 us
    psum x1, blocking collectives, per_device(): domain_total = lax.psum(domain_part, 'dp')  21.3 us
    all_gather x1, waiting for transfers between devices, per_device(): lax.all_gather(dense_portion, ('expert', 'tensor'))  20.1 us
    unnamed x5, waiting for transfers between devices  20.1 us
    reduce_scatter x1, waiting for transfers between devices, per_device(): lax.psum_scatter(jnp.einsum('lmtd,ldr->tlmr', block, dense_proj_in, prefe...  12.5 us
    dot_general x1, matrix products, per_device(): jnp.einsum('lmtd,ldr->tlmr', block, dense_proj_in, preferred_element_type...  6.62 us
    dot_general x1, matrix products, per_device(): jnp.einsum('lmtd,ldr->tlmr', dense_cot, dense_proj_out, preferred_element...  6.22 us
    dot_general x1, matrix products, per_device(): jnp.einsum('mecd,dr->cmer', expert_cot, expert_proj_out, preferred_elemen...  3.44 us
  transfers between devices with their start and end apart: 4, of which 4 were waited for; matrix products, arithmetic and copies ran while one was open for 15% of the time, Pallas kernels for 0%

profile of v1, /device:TPU:0, one launch (start us, length us, event | category | flops | bytes accessed | tf_op | source)
XLA Modules:
  0.0 165.1 jit_solution(10873097597282123408)
XLA Ops:
  6.5 0.0 copy-start
  6.5 0.0 copy-start.1
  6.5 0.0 all-reduce.6.cloned.1.call-start
  6.5 1.7 %copy-done = bf16[4,4,64,1280]{3,2,1,0:T(8,128)(2,1)S(1)} copy-done((bf16[4,4,64,1280]{3,2,1,0:T(8,128)(2,1)S(1)}, bf16[4,4,64,1280]{3,2,1,0:T(8,128)(2,1)}, u32[]{:S(2)}) %copy-start) | copy-done | bytes 2621464
  8.3 1.8 %convolution_bitcast_fusion.1 = f32[64,4,4,128]{3,0,2,1:T(8,128)S(1)} fusion(bf16[4,4,64,1280]{3,2,1,0:T(8,128)(2,1)S(1)} %copy-done, bf16[1280,128]{1,0:T(8,128)(2,1)} %param.18), kind=kOutput, calls=%fused_computation.4 | convolution fusion | flops 335544320 | bytes 3473408 | tf_op jit(solution)/shard_map/mecf,fr->cmer/dot_general | solution.py:36
  10.1 1.1 copy.16
  11.2 0.0 all-reduce.6.cloned.1.call-update
  11.3 0.0 copy-start.6
  11.3 0.0 reduce-scatter.2.cloned.1.call-start
  11.3 0.0 copy-done.1
  11.3 6.6 %convolution_bitcast_fusion = f32[256,2,4,128]{0,3,2,1:T(8,128)} fusion(bf16[2,4,256,1792]{3,2,1,0:T(8,128)(2,1)} %param.12, bf16[2,1792,128]{2,1,0:T(8,128)(2,1)S(1)} %copy-done.1), kind=kOutput, calls=%fused_computation.2 | convolution fusion | flops 939524096 | bytes 9306112 | tf_op jit(solution)/shard_map/lmtd,ldr->tlmr/dot_general | solution.py:23
  18.0 0.0 reduce-scatter.2.cloned.1.call-update
  18.0 0.0 all-reduce.4.cloned.1.call-start
  18.0 0.0 copy-done.6
  18.0 0.6 dynamic-slice
  19.3 3.4 %fusion.6 = f32[128,4,4,32]{0,3,2,1:T(8,128)S(1)} fusion(bf16[4,4,32,3584]{3,2,1,0:T(8,128)(2,1)} %param.17, bf16[3584,128]{1,0:T(8,128)(2,1)} %param.19), kind=kOutput, calls=%fused_computation.8 | convolution fusion | flops 469762048 | bytes 4849664 | tf_op jit(solution)/shard_map/mecd,dr->cmer/dot_general | solution.py:41
  22.7 20.1 %all-reduce.6.cloned.1.call-done = f32[64,4,4,128]{3,2,1,0:T(4,128)} async-done(((f32[64,4,4,128]{3,2,1,0:T(4,128)}), f32[64,4,4,128]{3,2,1,0:T(4,128)}) %all-reduce.6.cloned.1.call-update) | async-done | bytes 524304
  42.8 1.0 constant_dynamic-slice_fusion
  43.8 2.8 %fusion.9 = f32[4,4,128,128]{3,2,1,0:T(8,128)} fusion(f32[128,4,4,32]{0,3,2,1:T(8,128)S(1)} %fusion.6, f32[32,4,4,128]{3,2,1,0:T(4,128)S(1)} %constant_dynamic-slice_fusion), kind=kOutput, calls=%fused_computation.12 | convolution fusion | flops 100663296 | bytes 1572864 | tf_op jit(solution)/shard_map/cmer,cmes->mers/dot_general | solution.py:44
  46.6 0.0 all-reduce.4.cloned.1.call-update
  46.6 0.0 copy-start.2
  46.6 0.0 all-gather.3.cloned.1.call-start
  46.6 6.2 %fusion.2 = f32[128,2,4,128]{0,3,2,1:T(8,128)S(1)} fusion(bf16[2,4,128,3584]{3,2,1,0:T(8,128)(2,1)} %param.13, bf16[2,3584,128]{2,1,0:T(8,128)(2,1)} %param.15), kind=kOutput, calls=%fused_computation.3 | convolution fusion | flops 939524096 | bytes 9699328 | tf_op jit(solution)/shard_map/lmtd,ldr->tlmr/dot_general | solution.py:28
  52.9 0.0 copy-start.3
  52.9 0.0 copy-start.5
  52.9 0.0 copy-start.4
  52.9 12.5 %reduce-scatter.2.cloned.1.call-done = f32[128,2,4,128]{0,3,2,1:T(8,128)} async-done(((f32[256,2,4,128]{0,3,2,1:T(8,128)}), f32[128,2,4,128]{0,3,2,1:T(8,128)}) %reduce-scatter.2.cloned.1.call-update) | async-done | bytes 524304 | tf_op jit(solution)/shard_map/reduce_scatter | solution.py:22
  65.4 3.0 %fusion.12 = f32[2,4,128,128]{3,2,1,0:T(8,128)} fusion(f32[128,2,4,128]{0,3,2,1:T(8,128)} %reduce-scatter.2.cloned.1.call-done, f32[128,2,4,128]{0,3,2,1:T(8,128)S(1)} %fusion.2), kind=kOutput, calls=%fused_computation.22 | convolution fusion | flops 201326592 | bytes 1572864 | tf_op jit(solution)/shard_map/fquy,fquh->quyh/dot_general | solution.py:31
  68.5 0.0 all-gather.3.cloned.1.call-update
  68.5 39.3 %all-reduce.4.cloned.1.call-done = f32[4,4,128,128]{3,2,1,0:T(8,128)} async-done(((f32[4,4,128,128]{3,2,1,0:T(8,128)}), f32[4,4,128,128]{3,2,1,0:T(8,128)}) %all-reduce.4.cloned.1.call-update) | async-done | bytes 1048592 | tf_op jit(solution)/shard_map/psum | solution.py:49
  107.9 0.0 copy-done.2
  107.9 1.4 multiply_reduce_fusion
  109.3 2.4 %psum.22 = f32[4]{0:T(128)S(1)} all-reduce(f32[4]{0:T(128)S(1)} %multiply_reduce_fusion), channel_id=1, replica_groups=mesh['dp'=8,'expert'=2,'tensor'=2] {'expert'}, use_global_device_ids=true, to_apply=%region_6.0 | all-reduce | flops 4 | bytes 32 | tf_op jit(solution)/shard_map/psum | solution.py:51
  111.7 20.1 %all-gather.3.cloned.1.call-done = f32[8,4,128,128]{3,2,1,0:T(8,128)} async-done(((f32[2,4,128,128]{3,2,1,0:T(8,128)}), f32[8,4,128,128]{3,2,1,0:T(8,128)}) %all-gather.3.cloned.1.call-update) | async-done | bytes 2097168 | tf_op jit(solution)/shard_map/all_gather | solution.py:47
  131.9 1.8 %reduce_sum.45 = f32[2,4,128,128]{3,2,1,0:T(8,128)S(1)} reduce(f32[4,2,4,128,128]{4,3,2,1,0:T(8,128)} %bitcast.42, f32[]{:T(128)} %constant.7.clone.1), dimensions={0}, to_apply=%region_1.0 | reduce | flops 393216 | bytes 2621444 | tf_op jit(solution)/shard_map/reduce_sum | solution.py:47
  133.6 0.0 copy-done.3
  133.7 0.2 multiply_reduce_fusion.1
  133.8 0.0 copy-done.5
  133.8 0.2 convolution_bitcast_fusion.2
  134.0 21.3 %psum.23 = f32[64]{0:T(128)S(1)} all-reduce(f32[64]{0:T(128)S(1)} %convolution_bitcast_fusion.2), channel_id=1, replica_groups=mesh['dp'=8,'expert'=2,'tensor'=2] {'dp'}, use_global_device_ids=true, to_apply=%region_7.0 | all-reduce | flops 64 | bytes 512 | tf_op jit(solution)/shard_map/psum | solution.py:60
  155.3 0.6 multiply_reduce_fusion.3
  156.6 0.0 copy-done.4
  156.7 0.6 multiply_reduce_fusion.2
  158.0 0.6 add_subtract_fusion
Async XLA Ops:
  6.5 1.7 %copy-start = (bf16[4,4,64,1280]{3,2,1,0:T(8,128)(2,1)S(1)}, bf16[4,4,64,1280]{3,2,1,0:T(8,128)(2,1)}, u32[]{:S(2)}) copy-start(bf16[4,4,64,1280]{3,2,1,0:T(8,128)(2,1)} %param.16) | copy-start | bytes 7864324
  6.5 4.8 %copy-start.1 = (bf16[2,1792,128]{2,1,0:T(8,128)(2,1)S(1)}, bf16[2,1792,128]{2,1,0:T(8,128)(2,1)}, u32[]{:S(2)}) copy-start(bf16[2,1792,128]{2,1,0:T(8,128)(2,1)} %param.14) | copy-start | bytes 2752516
  6.5 36.3 %all-reduce.6.cloned.1.call-start = ((), (), s32[]{:S(2)}) async-start(), calls=%async_computation.4 | async-start | bytes 1048576
  11.3 6.8 %copy-start.6 = (u32[32]{0:T(128)S(1)}, u32[32]{0:T(128)}, u32[]{:S(2)}) copy-start(u32[32]{0:T(128)} %constant.29) | copy-start | bytes 388
  11.3 54.2 %reduce-scatter.2.cloned.1.call-start = ((), (), s32[]{:S(2)}) async-start(), calls=%async_computation.1 | async-start | bytes 1572864 | tf_op jit(solution)/shard_map/reduce_scatter | solution.py:22
  18.0 89.9 %all-reduce.4.cloned.1.call-start = ((), (), s32[]{:S(2)}) async-start(), calls=%async_computation.2 | async-start | bytes 2097152 | tf_op jit(solution)/shard_map/psum | solution.py:49
  46.6 61.3 %copy-start.2 = (f32[4,128,128]{2,1,0:T(8,128)S(1)}, f32[4,128,128]{2,1,0:T(8,128)}, u32[]{:S(2)}) copy-start(f32[4,128,128]{2,1,0:T(8,128)} %param.21) | copy-start | bytes 786436
  46.6 85.3 %all-gather.3.cloned.1.call-start = ((), (), s32[]{:S(2)}) async-start(), calls=%async_computation.3 | async-start | bytes 2621440 | tf_op jit(solution)/shard_map/all_gather | solution.py:47
  52.9 80.8 %copy-start.3 = (f32[2,128,128]{2,1,0:T(8,128)S(1)}, f32[2,128,128]{2,1,0:T(8,128)}, u32[]{:S(2)}) copy-start(f32[2,128,128]{2,1,0:T(8,128)} %param.20) | copy-start | bytes 393220
  52.9 80.9 %copy-start.5 = (s32[4]{0:T(128)S(1)}, s32[4]{0:T(128)}, u32[]{:S(2)}) copy-start(s32[4]{0:T(128)} %param.22) | copy-start | bytes 52
  52.9 103.7 %copy-start.4 = (f32[64]{0:T(128)S(1)}, f32[64]{0:T(128)}, u32[]{:S(2)}) copy-start(f32[64]{0:T(128)} %param.23) | copy-start | bytes 772
Sparse Core Ops, SparseCore 0:
  11.4 31.3 all-reduce.5
  45.0 20.3 reduce-scatter.1
  67.7 40.0 all-reduce.3
  109.3 22.5 all-gather.2
